TPU v7x, 8 devices: a whole 2x2x1 slice. The times are simulated.
8 devices in a mesh: dp: 2 (over y, z), tp: 4 (over x, core).
Axes of the slice: x: 2, y: 2, z: 1, core: 2. Of those that a mesh axis runs over, the one named last changes fastest.
Arguments:
- x: bfloat16 [256, 12288], P('dp'), parts along dimension 0
- w_gate: bfloat16 [12288, 28672], P(None, 'tp')
- w_up: bfloat16 [12288, 28672], P(None, 'tp')
- w_down: bfloat16 [28672, 12288], P('tp')
Outputs:
- output: bfloat16 [256, 12288], P('dp'), parts along dimension 0
There are 2 independent parts. A program takes and returns all parts, laid end to end along the dimension named above; an argument that names none is the same for every part.
All inputs are finite; a program needn't handle non-finite values.
Results may differ from a plain program's by a relative error of at most 0.016.
Values are sent between devices in bfloat16 or wider.
A program may use at most 2 GiB of HBM per device.

v0:
```python
import jax
import jax.numpy as jnp
from jax import lax
from jax.sharding import PartitionSpec as P


def solution(mesh):
    def step(x, w_gate, w_up, w_down):
        gate = jnp.dot(x, w_gate, preferred_element_type=jnp.float32)
        up = jnp.dot(x, w_up, preferred_element_type=jnp.float32)
        hidden = (jax.nn.silu(gate) * up).astype(jnp.bfloat16)
        term = jnp.dot(hidden, w_down, preferred_element_type=jnp.float32).astype(jnp.bfloat16)
        return lax.psum(term, "tp")

    return jax.shard_map(
        step,
        mesh=mesh,
        in_specs=(P("dp", None), P(None, "tp"), P(None, "tp"), P("tp", None)),
        out_specs=P("dp", None),
        check_vma=False,
    )
```

profile of v0, /device:TPU:0, one launch (start us, length us, event | category | flops | bytes accessed | tf_op | source)
XLA Modules:
  0.0 257.0 jit_solution(11719551811361004030)
XLA Ops:
  6.5 0.0 copy-start
  6.5 0.0 all-reduce.2.cloned.1.call-start
  6.5 1.9 copy-done
  8.4 56.8 %fusion.1 = f32[128,7168]{1,0:T(8,128)} fusion(bf16[128,12288]{1,0:T(8,128)(2,1)S(1)} %copy-done, bf16[12288,7168]{1,0:T(8,128)(2,1)} %param.5), kind=kOutput, calls=%fused_computation.3 | convolution fusion | flops 22548578304 | bytes 182976512 | tf_op jit(solution)/shard_map/dot_general | solution.py:9
  65.2 58.2 %fusion = bf16[128,7168]{1,0:T(8,128)(2,1)} fusion(bf16[128,12288]{1,0:T(8,128)(2,1)S(1)} %copy-done, bf16[12288,7168]{1,0:T(8,128)(2,1)} %param.6, f32[128,7168]{1,0:T(8,128)} %fusion.1), kind=kOutput, calls=%fused_computation.2 | convolution fusion | flops 22554083328 | bytes 184811520 | tf_op jit(solution)/shard_map/dot_general | solution.py:10
  123.4 57.2 %convolution_convert_fusion = bf16[128,12288]{1,0:T(8,128)(2,1)} fusion(bf16[128,7168]{1,0:T(8,128)(2,1)} %fusion, bf16[7168,12288]{1,0:T(8,128)(2,1)} %param.7), kind=kOutput, calls=%fused_computation | convolution fusion | flops 22550151168 | bytes 181141504 | tf_op jit(solution)/shard_map/dot_general | solution.py:12
  180.6 0.0 all-reduce.2.cloned.1.call-update
  180.6 65.7 %all-reduce.2.cloned.1.call-done = bf16[128,12288]{1,0:T(8,128)(2,1)} async-done(((bf16[128,12288]{1,0:T(8,128)(2,1)}), bf16[128,12288]{1,0:T(8,128)(2,1)}) %all-reduce.2.cloned.1.call-update) | async-done | bytes 3145744 | tf_op jit(solution)/shard_map/psum | solution.py:13
  246.3 3.8 %copy.6 = bf16[128,12288]{1,0:T(8,128)(2,1)} copy(bf16[128,12288]{1,0:T(8,128)(2,1)} %all-reduce.2.cloned.1.call-done) | data formatting | bytes 6291456
Async XLA Ops:
  6.5 1.9 copy-start
  6.5 239.7 %all-reduce.2.cloned.1.call-start = ((), (), s32[]{:S(2)}) async-start(), calls=%async_computation | async-start | bytes 6291456 | tf_op jit(solution)/shard_map/psum | solution.py:13
Sparse Core Ops, SparseCore 0:
  180.7 65.5 all-reduce.1
where the time goes:
time: 257 us
  matrix products  172 us (67%)
  waiting for transfers between devices  65.7 us (26%)
  between operations  13.4 us (5%)
  local copies, waits for them, and re-layouts  5.72 us (2%)
    psum x1, waiting for transfers between devices, step(): return lax.psum(term, 'tp')  65.7 us
    dot_general x1, matrix products, step(): up = jnp.dot(x, w_up, preferred_element_type=jnp.float32)  58.2 us
    dot_general x1, matrix products, step(): jnp.dot(hidden, w_down, preferred_element_type=jnp.float32)  57.2 us
    dot_general x1, matrix products, step(): gate = jnp.dot(x, w_gate, preferred_element_type=jnp.float32)  56.8 us
    unnamed x3, local copies, waits for them, and re-layouts  5.72 us
  transfers between devices with their start and end apart: 1, of which 1 were waited for; matrix products, arithmetic and copies ran while one was open for 0% of the time, Pallas kernels for 0%

commit v1 on v0

v1 whole, which is shorter than its diff:
```python
import functools

import jax
import jax.numpy as jnp
from jax import lax
from jax.experimental import pallas as pl
from jax.experimental.pallas import tpu as pltpu
from jax.sharding import PartitionSpec as P

MESH = pl.DeviceIdType.MESH
F32 = jnp.float32
BF16 = jnp.bfloat16

KC = 512
NC = 512
SLOTS = 8
LAG_B, LAG_C, LAG_D = 1, 4, 7


def kernel(
    x_ref, wg_ref, wu_ref, wd_ref, y_ref,
    xb, w, acc_g, acc_u, hid, keep, mine, a_out, a_in, b_out, b_in, c_out, c_in, fin,
    x_load, x_send, x_recv, f_send, f_recv, w_sem,
    a_send, a_recv, b_send, b_recv, c_send, c_recv, d_send, d_recv, d_local,
):
    rows, depth = x_ref.shape
    steps = depth // KC
    blocks = w.shape[1]
    half_ff = blocks * NC
    half = NC // 2
    side = depth // 2
    chunks = side // half
    part = rows // 2

    dp, tp = lax.axis_index("dp"), lax.axis_index("tp")
    core = lax.rem(tp, 2)
    over_core = {"dp": dp, "tp": tp + 1 - 2 * core}
    over_y = {"dp": 1 - dp, "tp": tp}
    over_x = {"dp": dp, "tp": lax.rem(tp + 2, 4)}

    def load_x(s):
        cols = pl.ds(pl.multiple_of(s * KC, KC), KC)
        return pltpu.make_async_copy(x_ref.at[:, cols], xb.at[s, pl.ds(0, rows), :], x_load.at[s])

    def send_x(s):
        src = xb.at[s, pl.ds(pl.multiple_of(part * core, part), part), :]
        dst = xb.at[s, pl.ds(pl.multiple_of(rows + part * core, part), part), :]
        return pltpu.make_async_remote_copy(
            src, dst, x_send.at[s], x_recv.at[s], device_id=over_y, device_id_type=MESH)

    def forward_x(s):
        ref = xb.at[s, pl.ds(pl.multiple_of(rows + part * core, part), part), :]
        return pltpu.make_async_remote_copy(
            ref, ref, f_send.at[s], f_recv.at[s], device_id=over_core, device_id_type=MESH)

    def load_in(src_ref, s, slot):
        for j in range(blocks):
            cols = pl.ds(pl.multiple_of(half_ff * dp + j * NC, NC), NC)
            pltpu.make_async_copy(
                src_ref.at[pl.ds(pl.multiple_of(s * KC, KC), KC), cols], w.at[slot, j], w_sem.at[slot]).start()

    def load_down(n, slot):
        for i, owner in enumerate((core, 1 - core)):
            cols = pl.ds(pl.multiple_of(side * owner + half * n, half), half)
            pltpu.make_async_copy(
                wd_ref.at[pl.ds(blocks * dp, blocks), :, cols],
                w.at[slot, :, :, pl.ds(i * half, half)], w_sem.at[slot]).start()

    def wait_w(slot):
        pltpu.make_async_copy(w.at[slot], w.at[slot], w_sem.at[slot]).wait()

    def a_copy(n):
        return pltpu.make_async_remote_copy(
            a_out.at[n], a_in.at[n], a_send.at[n], a_recv.at[n], device_id=over_core, device_id_type=MESH)

    def b_copy(n):
        return pltpu.make_async_remote_copy(
            b_out.at[n], b_in.at[n], b_send.at[n], b_recv.at[n], device_id=over_y, device_id_type=MESH)

    def c_copy(n):
        return pltpu.make_async_remote_copy(
            c_out.at[n], c_in.at[n], c_send.at[n], c_recv.at[n], device_id=over_x, device_id_type=MESH)

    def d_cols(owner, n):
        return y_ref.at[:, pl.ds(pl.multiple_of(side * owner + half * n, half), half)]

    def d_copy(n):
        return pltpu.make_async_remote_copy(
            fin.at[n], d_cols(core, n), d_send.at[n], d_recv.at[n], device_id=over_core, device_id_type=MESH)

    def d_keep(n):
        return pltpu.make_async_copy(fin.at[n], d_cols(core, n), d_local.at[n])

    def loop(lo, hi, body):
        def run(i, carry):
            body(i)
            return carry

        lax.fori_loop(lo, hi, run, 0)

    loop(0, steps, lambda s: load_x(s).start())
    for s in range(SLOTS // 2):
        load_in(wg_ref, s, 2 * s)
        load_in(wu_ref, s, 2 * s + 1)
    barrier = pltpu.get_barrier_semaphore()
    for other in (over_core, over_y, over_x):
        pl.semaphore_signal(barrier, inc=1, device_id=other, device_id_type=MESH)
    pl.semaphore_wait(barrier, 3)

    def first(s):
        load_x(s).wait()
        send_x(s).start()

    loop(0, steps, first)
    acc_g[...] = jnp.zeros_like(acc_g)
    acc_u[...] = jnp.zeros_like(acc_u)
    send_x(0).wait_recv()
    forward_x(0).start()

    def refill(s, slot, src_ref, odd):
        @pl.when(s + SLOTS // 2 < steps)
        def _():
            load_in(src_ref, s + SLOTS // 2, slot)

        @pl.when(s + SLOTS // 2 >= steps)
        def _():
            load_down(2 * (s + SLOTS // 2 - steps) + odd, slot)

    def project(s):
        @pl.when(s + 1 < steps)
        def _():
            send_x(s + 1).wait_recv()
            forward_x(s + 1).start()

        forward_x(s).wait_recv()
        for odd, (src_ref, acc) in enumerate(((wg_ref, acc_g), (wu_ref, acc_u))):
            slot = lax.rem(2 * s + odd, SLOTS)
            wait_w(slot)
            for j in range(blocks):
                acc[j] += jnp.dot(xb[s], w[slot, j], preferred_element_type=F32)
            refill(s, slot, src_ref, odd)

    loop(0, steps, project)

    for j in range(blocks):
        hid[:, j * NC:(j + 1) * NC] = (jax.nn.silu(acc_g[j]) * acc_u[j]).astype(BF16)

    def finish(n):
        @pl.when(n < chunks)
        def _():
            slot = lax.rem(n, SLOTS)
            wait_w(slot)
            term = jnp.dot(hid[...], w[slot].reshape(half_ff, NC), preferred_element_type=F32)
            a_out[n] = term[:, half:].astype(BF16)
            keep[lax.rem(n, LAG_B + 1)] = term[:, :half]
            a_copy(n).start()

            @pl.when(n + SLOTS < chunks)
            def _():
                load_down(n + SLOTS, slot)

        b = n - LAG_B

        @pl.when((b >= 0) & (b < chunks))
        def _():
            a_copy(b).wait_recv()
            total = keep[lax.rem(b, LAG_B + 1)] + a_in[b].astype(F32)
            b_out[b] = total[rows:].astype(BF16)
            mine[b] = total[:rows]
            b_copy(b).start()

        c = n - LAG_C

        @pl.when((c >= 0) & (c < chunks))
        def _():
            b_copy(c).wait_recv()
            c_out[c] = (mine[c] + b_in[c].astype(F32)).astype(BF16)
            c_copy(c).start()

        d = n - LAG_D

        @pl.when(d >= 0)
        def _():
            c_copy(d).wait_recv()
            fin[d] = (c_out[d].astype(F32) + c_in[d].astype(F32)).astype(BF16)
            d_copy(d).start()
            d_keep(d).start()

    loop(0, chunks + LAG_D, finish)

    def last_x(s):
        send_x(s).wait_send()
        forward_x(s).wait_send()

    def last(n):
        a_copy(n).wait_send()
        b_copy(n).wait_send()
        c_copy(n).wait_send()
        d_keep(n).wait()
        d_copy(n).wait()

    loop(0, steps, last_x)
    loop(0, chunks, last)


def solution(mesh):
    def step(x, w_gate, w_up, w_down):
        rows, depth = x.shape
        ff = w_gate.shape[1]
        blocks = ff // 2 // NC
        steps = depth // KC
        half = NC // 2
        chunks = depth // NC
        dma = pltpu.SemaphoreType.DMA
        hbm = pl.BlockSpec(memory_space=pl.ANY)
        return pl.pallas_call(
            kernel,
            out_shape=jax.ShapeDtypeStruct((rows, depth), BF16),
            in_specs=[hbm] * 4,
            out_specs=hbm,
            scratch_shapes=[
                pltpu.VMEM((steps, 2 * rows, KC), BF16),
                pltpu.VMEM((SLOTS, blocks, KC, NC), BF16),
                pltpu.VMEM((blocks, 2 * rows, NC), F32),
                pltpu.VMEM((blocks, 2 * rows, NC), F32),
                pltpu.VMEM((2 * rows, blocks * NC), BF16),
                pltpu.VMEM((LAG_B + 1, 2 * rows, half), F32),
                pltpu.VMEM((chunks, rows, half), F32),
                pltpu.VMEM((chunks, 2 * rows, half), BF16),
                pltpu.VMEM((chunks, 2 * rows, half), BF16),
                pltpu.VMEM((chunks, rows, half), BF16),
                pltpu.VMEM((chunks, rows, half), BF16),
                pltpu.VMEM((chunks, rows, half), BF16),
                pltpu.VMEM((chunks, rows, half), BF16),
                pltpu.VMEM((chunks, rows, half), BF16),
                dma((steps,)), dma((steps,)), dma((steps,)), dma((steps,)), dma((steps,)), dma((SLOTS,)),
                dma((chunks,)), dma((chunks,)), dma((chunks,)), dma((chunks,)), dma((chunks,)), dma((chunks,)),
                dma((chunks,)), dma((chunks,)), dma((chunks,)),
            ],
            compiler_params=pltpu.CompilerParams(
                collective_id=0, has_side_effects=True, vmem_limit_bytes=67_000_000),
        )(x, w_gate, w_up, w_down.reshape(ff // NC, NC, depth))

    return jax.shard_map(
        step,
        mesh=mesh,
        in_specs=(P("dp", None), P(None, "tp"), P(None, "tp"), P("tp", None)),
        out_specs=P("dp", None),
        check_vma=False,
    )
```

time: 257 us -> 114 us (0.44)
  matrix products: 172 us -> 0 us
  Pallas kernels: 0 us -> 110 us
  waiting for transfers between devices: 65.7 us -> 0 us
  between operations: 13.4 us -> 0.01 us
    dot_general x3 -> x0, matrix products: 172 us -> none  [the longest x1 58.2 us: step(): up = jnp.dot(x, w_up, preferred_element_type=jnp.float32)]
    pallas_call x0 -> x1, Pallas kernels: none -> 110 us  [step(): pl.pallas_call(kernel, out_shape=jax.ShapeDtypeStruct((rows, depth), BF16...]
    psum x1 -> x0, waiting for transfers between devices: 65.7 us -> none  [step(): return lax.psum(term, 'tp')]
    unnamed x3 -> x1, local copies, waits for them, and re-layouts: 5.72 us -> 3.83 us
  transfers between devices with their start and end apart: 1 -> 0, of which waited for: 1 -> 0; matrix products, arithmetic and copies ran while one was open for 0% -> 0% of each run, Pallas kernels for 0% -> 0%
where the time goes in v1:
time: 114 us
  Pallas kernels  110 us (96%)
  local copies, waits for them, and re-layouts  3.83 us (3%)
    pallas_call x1, Pallas kernels, step(): pl.pallas_call(kernel, out_shape=jax.ShapeDtypeStruct((rows, depth), BF16...  110 us
    unnamed x1, local copies, waits for them, and re-layouts  3.83 us

profile of v1, /device:TPU:0, one launch (start us, length us, event | category | flops | bytes accessed | tf_op | source)
XLA Modules:
  0.0 113.7 jit_solution(7130718782909134202)
XLA Ops:
  0.0 109.8 %shard_map.46 = bf16[128,12288]{1,0:T(8,128)(2,1)} custom-call(bf16[128,12288]{1,0:T(8,128)(2,1)} %x_ref.1, bf16[12288,7168]{1,0:T(8,128)(2,1)} %wg_ref.1, bf16[12288,7168]{1,0:T(8,128)(2,1)} %wu_ref.1, bf16[14,512,12288]{2,1,0:T(8,128)(2,1)} %bitcast.wd_ref), custom_call_target="tpu_custom_call" | custom-call | tf_op jit(solution)/shard_map/pallas_call | solution.py:216
  109.8 3.8 %copy.6 = bf16[128,12288]{1,0:T(8,128)(2,1)} copy(bf16[128,12288]{1,0:T(8,128)(2,1)} %shard_map.46) | data formatting | bytes 6291456

commit v2 on v0

v2 whole, which is shorter than its diff:
```python
import functools

import jax
import jax.numpy as jnp
from jax import lax
from jax.experimental import pallas as pl
from jax.experimental.pallas import tpu as pltpu
from jax.sharding import PartitionSpec as P

MESH = pl.DeviceIdType.MESH
F32 = jnp.float32
BF16 = jnp.bfloat16

KC = 512
NC = 512
SUB = 256
PER = NC // (2 * SUB)
SLOTS = 10
EARLY = 2
SINGLES = 6
LAG_B, LAG_C, LAG_D = 1, 4, 7
RING_A, RING_B, RING_C = 4, 8, 8


def kernel(
    x_ref, wg_ref, wu_ref, wd_ref, y_ref,
    xb, w, acc_g, acc_u, hid, a_in, b_in, c_in,
    x_load, x_send, x_recv, f_send, f_recv, w_sem,
    a_send, a_recv, b_send, b_recv, c_send, c_recv, d_send, d_recv,
):
    rows, depth = x_ref.shape
    steps = depth // KC
    blocks = w.shape[1]
    half_ff = blocks * NC
    side = depth // 2
    units = depth // NC
    part = rows // 2
    both = (0, 2 * rows)

    dp, tp = lax.axis_index("dp"), lax.axis_index("tp")
    core = lax.rem(tp, 2)
    over_core = {"dp": dp, "tp": tp + 1 - 2 * core}
    over_y = {"dp": 1 - dp, "tp": tp}
    over_x = {"dp": dp, "tp": lax.rem(tp + 2, 4)}

    def load_x(s):
        cols = pl.ds(pl.multiple_of(s * KC, KC), KC)
        which = (s >= SINGLES).astype(jnp.int32)
        return pltpu.make_async_copy(x_ref.at[:, cols], xb.at[s, pl.ds(0, rows), :], x_load.at[which])

    def loaded_x(first, count, which):
        ref = xb.at[pl.ds(first, count), pl.ds(0, rows), :]
        pltpu.make_async_copy(ref, ref, x_load.at[which]).wait()

    def x_part(base, s, count):
        return xb.at[pl.ds(s, count), pl.ds(pl.multiple_of(base + part * core, part), part), :]

    def x_sem(s, count):
        return s if count == 1 else SINGLES + (s - SINGLES) // 2

    def send_x(s, count):
        return pltpu.make_async_remote_copy(
            x_part(0, s, count), x_part(rows, s, count), x_send.at[0], x_recv.at[x_sem(s, count)],
            device_id=over_y, device_id_type=MESH)

    def forward_x(s, count):
        ref = x_part(rows, s, count)
        return pltpu.make_async_remote_copy(
            ref, ref, f_send.at[0], f_recv.at[x_sem(s, count)], device_id=over_core, device_id_type=MESH)

    def load_in(src_ref, s, slot):
        for j in range(blocks):
            cols = pl.ds(pl.multiple_of(half_ff * dp + j * NC, NC), NC)
            pltpu.make_async_copy(
                src_ref.at[pl.ds(pl.multiple_of(s * KC, KC), KC), cols], w.at[slot, j], w_sem.at[slot]).start()

    def load_down(n, slot):
        for sub in range(PER):
            for i, owner in enumerate((core, 1 - core)):
                cols = pl.ds(pl.multiple_of(side * owner + PER * SUB * n + SUB * sub, SUB), SUB)
                pltpu.make_async_copy(
                    wd_ref.at[pl.ds(blocks * dp, blocks), :, cols],
                    w.at[slot, :, :, pl.ds((2 * sub + i) * SUB, SUB)], w_sem.at[slot]).start()

    def wait_w(slot):
        pltpu.make_async_copy(w.at[slot], w.at[slot], w_sem.at[slot]).wait()

    def a_out(n, sub):
        return xb.at[n, :, pl.ds(2 * SUB * sub, SUB)]

    def b_out(n, sub):
        return xb.at[n, pl.ds(0, rows), pl.ds(2 * SUB * sub + SUB, SUB)]

    def c_out(n, sub):
        return xb.at[n, pl.ds(rows, rows), pl.ds(2 * SUB * sub + SUB, SUB)]

    def keep(n, sub):
        return acc_u.at[lax.rem(n, blocks), :, pl.ds(SUB * sub, SUB)]

    def mine(n, sub):
        return acc_g.at[lax.rem(n, blocks), pl.ds(0, rows), pl.ds(SUB * sub, SUB)]

    def a_copy(n, sub):
        m = PER * n + sub
        return pltpu.make_async_remote_copy(
            a_out(n, sub), a_in.at[m], a_send.at[0], a_recv.at[lax.rem(m, RING_A)],
            device_id=over_core, device_id_type=MESH)

    def b_copy(n, sub):
        m = PER * n + sub
        return pltpu.make_async_remote_copy(
            b_out(n, sub), b_in.at[m], b_send.at[0], b_recv.at[lax.rem(m, RING_B)],
            device_id=over_y, device_id_type=MESH)

    def c_copy(n, sub):
        m = PER * n + sub
        return pltpu.make_async_remote_copy(
            c_out(n, sub), c_in.at[m], c_send.at[0], c_recv.at[lax.rem(m, RING_C)],
            device_id=over_x, device_id_type=MESH)

    def d_cols(n, sub):
        return y_ref.at[:, pl.ds(pl.multiple_of(side * core + PER * SUB * n + SUB * sub, SUB), SUB)]

    def d_copy(n, sub):
        ref = d_cols(n, sub)
        return pltpu.make_async_remote_copy(
            ref, ref, d_send.at[0], d_recv.at[0], device_id=over_core, device_id_type=MESH)

    def loop(lo, hi, body):
        def run(i, carry):
            body(i)
            return carry

        lax.fori_loop(lo, hi, run, 0)

    barrier = pltpu.get_barrier_semaphore()
    for other in (over_core, over_y, over_x):
        pl.semaphore_signal(barrier, inc=1, device_id=other, device_id_type=MESH)
    loop(0, steps, lambda s: load_x(s).start())

    ins = ((wg_ref, acc_g), (wu_ref, acc_u))

    def slot_in(s, which):
        return lax.rem(2 * s + which, SLOTS)

    def slot_down(n):
        return lax.rem(2 * steps + n, SLOTS)

    for s in range(SLOTS // 2):
        for which in range(2):
            load_in(ins[which][0], s, slot_in(s, which))
    acc_g[...] = jnp.zeros_like(acc_g)
    acc_u[...] = jnp.zeros_like(acc_u)
    pl.semaphore_wait(barrier, 3)

    loaded_x(0, SINGLES, 0)
    loop(0, SINGLES, lambda s: send_x(s, 1).start())
    loaded_x(SINGLES, steps - SINGLES, 1)
    loop(SINGLES // 2, steps // 2, lambda step: send_x(2 * step, 2).start())

    def project(s, count, span, wait=True, free=True, last=False):
        lo, size = span
        if wait:
            for which in range(2):
                for i in range(count):
                    wait_w(slot_in(s + i, which))
        for which, (src_ref, acc) in enumerate(ins):
            for j in range(blocks):
                total = acc[j, lo:lo + size, :]
                for i in range(count):
                    total += jnp.dot(
                        xb[s + i, lo:lo + size, :], w[slot_in(s + i, which), j], preferred_element_type=F32)
                acc[j, lo:lo + size, :] = total
            for i in range(count if free else 0):
                ahead = s + i + SLOTS // 2
                slot = slot_in(s + i, which)
                if not last:
                    load_in(src_ref, ahead, slot)
                    continue

                @pl.when(ahead < steps)
                def _():
                    load_in(src_ref, ahead, slot)

                @pl.when(ahead >= steps)
                def _():
                    load_down(2 * (ahead - steps) + which, slot)

    def take_x(s, count):
        send_x(s, count).wait_recv()
        forward_x(s, count).start()

    loop(0, EARLY, lambda s: project(s, 1, (0, rows), free=False))
    take_x(0, 1)

    def late(s):
        take_x(s + 1, 1)
        forward_x(s, 1).wait_recv()
        project(s, 1, (rows, rows), wait=False)

    loop(0, EARLY, late)

    def single(s):
        @pl.when(s + 1 < SINGLES)
        def _():
            take_x(s + 1, 1)

        @pl.when(s + 1 == SINGLES)
        def _():
            take_x(SINGLES, 2)

        forward_x(s, 1).wait_recv()
        project(s, 1, both)

    loop(EARLY, SINGLES, single)

    def double(s, last):
        @pl.when(s + 2 < steps)
        def _():
            take_x(s + 2, 2)

        forward_x(s, 2).wait_recv()
        project(s, 2, both, last=last)

    tail = (steps - SLOTS // 2) // 2 * 2
    loop(SINGLES // 2, tail // 2, lambda step: double(2 * step, False))
    loop(tail // 2, steps // 2, lambda step: double(2 * step, True))

    whole = xb.at[:, pl.ds(0, part), :]
    for sem in (x_send, f_send):
        pltpu.make_async_copy(whole, whole, sem.at[0]).wait()
    for j in range(blocks):
        hid[:, j * NC:(j + 1) * NC] = (jax.nn.silu(acc_g[j]) * acc_u[j]).astype(BF16)

    def finish(n):
        for sub in range(PER):
            @pl.when(n < units)
            def _():
                slot = slot_down(n)
                if sub == 0:
                    wait_w(slot)
                cols = w[slot, :, :, 2 * SUB * sub:2 * SUB * (sub + 1)].reshape(half_ff, 2 * SUB)
                term = jnp.dot(hid[...], cols, preferred_element_type=F32)
                a_out(n, sub)[...] = term[:, SUB:].astype(BF16)
                keep(n, sub)[...] = term[:, :SUB]
                a_copy(n, sub).start()
                if sub == PER - 1:
                    @pl.when(n + SLOTS < units)
                    def _():
                        load_down(n + SLOTS, slot)

            b = n - LAG_B // PER

            @pl.when((b >= 0) & (b < units))
            def _():
                a_copy(b, sub).wait_recv()
                total = keep(b, sub)[...] + a_in[PER * b + sub].astype(F32)
                b_out(b, sub)[...] = total[rows:].astype(BF16)
                mine(b, sub)[...] = total[:rows]
                b_copy(b, sub).start()

            c = n - LAG_C // PER

            @pl.when((c >= 0) & (c < units))
            def _():
                b_copy(c, sub).wait_recv()
                c_out(c, sub)[...] = (mine(c, sub)[...] + b_in[PER * c + sub].astype(F32)).astype(BF16)
                c_copy(c, sub).start()

            d = n - LAG_D // PER

            @pl.when(d >= 0)
            def _():
                c_copy(d, sub).wait_recv()
                m = PER * d + sub
                d_cols(d, sub)[...] = (c_out(d, sub)[...].astype(F32) + c_in[m].astype(F32)).astype(BF16)
                d_copy(d, sub).start()

    loop(0, units + LAG_D // PER, finish)

    whole = xb.at[:, :, pl.ds(0, PER * SUB)]
    pltpu.make_async_copy(whole, whole, a_send.at[0]).wait()
    whole = xb.at[:, pl.ds(0, rows), pl.ds(0, PER * SUB)]
    for sem in (b_send, c_send, d_send, d_recv):
        pltpu.make_async_copy(whole, whole, sem.at[0]).wait()


def solution(mesh):
    def step(x, w_gate, w_up, w_down):
        rows, depth = x.shape
        ff = w_gate.shape[1]
        blocks = ff // 2 // NC
        steps = depth // KC
        pieces = depth // (2 * SUB)
        waves = SINGLES + (steps - SINGLES) // 2
        dma = pltpu.SemaphoreType.DMA
        hbm = pl.BlockSpec(memory_space=pl.ANY)
        return pl.pallas_call(
            kernel,
            out_shape=pltpu.VMEM((rows, depth), BF16),
            in_specs=[hbm] * 4,
            out_specs=pl.BlockSpec(memory_space=pltpu.VMEM),
            scratch_shapes=[
                pltpu.VMEM((steps, 2 * rows, KC), BF16),
                pltpu.VMEM((SLOTS, blocks, KC, NC), BF16),
                pltpu.VMEM((blocks, 2 * rows, NC), F32),
                pltpu.VMEM((blocks, 2 * rows, NC), F32),
                pltpu.VMEM((2 * rows, blocks * NC), BF16),
                pltpu.VMEM((pieces, 2 * rows, SUB), BF16),
                pltpu.VMEM((pieces, rows, SUB), BF16),
                pltpu.VMEM((pieces, rows, SUB), BF16),
                dma((2,)), dma((1,)), dma((waves,)), dma((1,)), dma((waves,)), dma((SLOTS,)),
                dma((1,)), dma((RING_A,)), dma((1,)), dma((RING_B,)), dma((1,)), dma((RING_C,)),
                dma((1,)), dma((1,)),
            ],
            compiler_params=pltpu.CompilerParams(
                collective_id=0, has_side_effects=True, vmem_limit_bytes=61_000_000),
        )(x, w_gate, w_up, w_down.reshape(ff // NC, NC, depth))

    return jax.shard_map(
        step,
        mesh=mesh,
        in_specs=(P("dp", None), P(None, "tp"), P(None, "tp"), P("tp", None)),
        out_specs=P("dp", None),
        check_vma=False,
    )
```

time: 257 us -> 107 us (0.42)
  matrix products: 172 us -> 0 us
  Pallas kernels: 0 us -> 105 us
  waiting for transfers between devices: 65.7 us -> 0 us
  between operations: 13.4 us -> 0.01 us
  local copies, waits for them, and re-layouts: 5.72 us -> 1.67 us
    dot_general x3 -> x0, matrix products: 172 us -> none  [the longest x1 58.2 us: step(): up = jnp.dot(x, w_up, preferred_element_type=jnp.float32)]
    pallas_call x0 -> x1, Pallas kernels: none -> 105 us  [step(): pl.pallas_call(kernel, out_shape=pltpu.VMEM((rows, depth), BF16), in_spec...]
    psum x1 -> x0, waiting for transfers between devices: 65.7 us -> none  [step(): return lax.psum(term, 'tp')]
    unnamed x3 -> x1, local copies, waits for them, and re-layouts: 5.72 us -> 1.67 us
  transfers between devices with their start and end apart: 1 -> 0, of which waited for: 1 -> 0; matrix products, arithmetic and copies ran while one was open for 0% -> 0% of each run, Pallas kernels for 0% -> 0%
where the time goes in v2:
time: 107 us
  Pallas kernels  105 us (98%)
  local copies, waits for them, and re-layouts  1.67 us (2%)
    pallas_call x1, Pallas kernels, step(): pl.pallas_call(kernel, out_shape=pltpu.VMEM((rows, depth), BF16), in_spec...  105 us

profile of v2, /device:TPU:0, one launch (start us, length us, event | category | flops | bytes accessed | tf_op | source)
XLA Modules:
  0.0 107.0 jit_solution(7232100792037385740)
XLA Ops:
  0.0 105.3 %shard_map.46 = bf16[128,12288]{1,0:T(8,128)(2,1)S(1)} custom-call(bf16[128,12288]{1,0:T(8,128)(2,1)} %x_ref.1, bf16[12288,7168]{1,0:T(8,128)(2,1)} %wg_ref.1, bf16[12288,7168]{1,0:T(8,128)(2,1)} %wu_ref.1, bf16[14,512,12288]{2,1,0:T(8,128)(2,1)} %bitcast.wd_ref), custom_call_target="tpu_custom_call" | custom-call | tf_op jit(solution)/shard_map/pallas_call | solution.py:298
  105.3 1.7 %copy.6 = bf16[128,12288]{1,0:T(8,128)(2,1)} copy(bf16[128,12288]{1,0:T(8,128)(2,1)S(1)} %shard_map.46) | data formatting | bytes 6291456

commit v3 on v2

--- a/solution.py
+++ b/solution.py
@@ -13,13 +13,13 @@
 
 KC = 512
 NC = 512
-SUB = 256
+SUB = 128
 PER = NC // (2 * SUB)
 SLOTS = 10
-EARLY = 2
-SINGLES = 6
+EARLY = 3
+SINGLES = 8
 LAG_B, LAG_C, LAG_D = 1, 4, 7
-RING_A, RING_B, RING_C = 4, 8, 8
+RING_A, RING_B, RING_C = 8, 16, 16
 
 
 def kernel(
@@ -158,125 +158,133 @@
     loaded_x(SINGLES, steps - SINGLES, 1)
     loop(SINGLES // 2, steps // 2, lambda step: send_x(2 * step, 2).start())
 
-    def project(s, count, span, wait=True, free=True, last=False):
+    def project(s, span, wait=True, each=False, refill=None):
         lo, size = span
-        if wait:
+        if wait and not each:
             for which in range(2):
-                for i in range(count):
-                    wait_w(slot_in(s + i, which))
+                wait_w(slot_in(s, which))
         for which, (src_ref, acc) in enumerate(ins):
+            slot = slot_in(s, which)
+            if each:
+                wait_w(slot)
             for j in range(blocks):
-                total = acc[j, lo:lo + size, :]
-                for i in range(count):
-                    total += jnp.dot(
-                        xb[s + i, lo:lo + size, :], w[slot_in(s + i, which), j], preferred_element_type=F32)
-                acc[j, lo:lo + size, :] = total
-            for i in range(count if free else 0):
-                ahead = s + i + SLOTS // 2
-                slot = slot_in(s + i, which)
-                if not last:
-                    load_in(src_ref, ahead, slot)
-                    continue
-
-                @pl.when(ahead < steps)
-                def _():
-                    load_in(src_ref, ahead, slot)
-
-                @pl.when(ahead >= steps)
-                def _():
-                    load_down(2 * (ahead - steps) + which, slot)
+                acc[j, lo:lo + size, :] += jnp.dot(
+                    xb[s, lo:lo + size, :], w[slot, j], preferred_element_type=F32)
+            ahead = s + SLOTS // 2
+            if refill == "in":
+                load_in(src_ref, ahead, slot)
+            elif refill == "down":
+                load_down(2 * (ahead - steps) + which, slot)
 
     def take_x(s, count):
         send_x(s, count).wait_recv()
         forward_x(s, count).start()
 
-    loop(0, EARLY, lambda s: project(s, 1, (0, rows), free=False))
-    take_x(0, 1)
+    def own(s):
+        project(s, (0, rows), each=True)
+
+        @pl.when(s > 0)
+        def _():
+            take_x(s - 1, 1)
+
+    loop(0, EARLY, own)
 
     def late(s):
-        take_x(s + 1, 1)
         forward_x(s, 1).wait_recv()
-        project(s, 1, (rows, rows), wait=False)
+        project(s, (rows, rows), wait=False, refill="in")
+        take_x(s + EARLY - 1, 1)
 
     loop(0, EARLY, late)
 
     def single(s):
-        @pl.when(s + 1 < SINGLES)
-        def _():
-            take_x(s + 1, 1)
-
-        @pl.when(s + 1 == SINGLES)
+        @pl.when(s + 2 < SINGLES)
+        def _():
+            take_x(s + 2, 1)
+
+        @pl.when(s + 2 == SINGLES)
         def _():
             take_x(SINGLES, 2)
 
         forward_x(s, 1).wait_recv()
-        project(s, 1, both)
+        project(s, both, refill="in")
 
     loop(EARLY, SINGLES, single)
 
-    def double(s, last):
-        @pl.when(s + 2 < steps)
+    def paired(s, refill):
+        even = lax.rem(s, 2) == 0
+
+        @pl.when(even & (s + 2 < steps))
         def _():
             take_x(s + 2, 2)
 
-        forward_x(s, 2).wait_recv()
-        project(s, 2, both, last=last)
-
-    tail = (steps - SLOTS // 2) // 2 * 2
-    loop(SINGLES // 2, tail // 2, lambda step: double(2 * step, False))
-    loop(tail // 2, steps // 2, lambda step: double(2 * step, True))
+        @pl.when(even)
+        def _():
+            forward_x(s, 2).wait_recv()
+
+        project(s, both, refill=refill)
+
+    loop(SINGLES, steps - SLOTS // 2, lambda s: paired(s, "in"))
+    loop(steps - SLOTS // 2, steps, lambda s: paired(s, "down"))
 
     whole = xb.at[:, pl.ds(0, part), :]
     for sem in (x_send, f_send):
         pltpu.make_async_copy(whole, whole, sem.at[0]).wait()
+    def down(n):
+        term = jnp.dot(hid[...], w[slot_down(n)].reshape(half_ff, NC), preferred_element_type=F32)
+        for sub in range(PER):
+            lo = 2 * SUB * sub
+            a_out(n, sub)[...] = term[:, lo + SUB:lo + 2 * SUB].astype(BF16)
+            keep(n, sub)[...] = term[:, lo:lo + SUB]
+        for sub in range(PER):
+            a_copy(n, sub).start()
+
+    wait_w(slot_down(0))
     for j in range(blocks):
         hid[:, j * NC:(j + 1) * NC] = (jax.nn.silu(acc_g[j]) * acc_u[j]).astype(BF16)
+    down(0)
+    load_down(SLOTS, slot_down(0))
 
     def finish(n):
-        for sub in range(PER):
-            @pl.when(n < units)
+        @pl.when(n < units)
+        def _():
+            wait_w(slot_down(n))
+            down(n)
+
+            @pl.when(n + SLOTS < units)
             def _():
-                slot = slot_down(n)
-                if sub == 0:
-                    wait_w(slot)
-                cols = w[slot, :, :, 2 * SUB * sub:2 * SUB * (sub + 1)].reshape(half_ff, 2 * SUB)
-                term = jnp.dot(hid[...], cols, preferred_element_type=F32)
-                a_out(n, sub)[...] = term[:, SUB:].astype(BF16)
-                keep(n, sub)[...] = term[:, :SUB]
-                a_copy(n, sub).start()
-                if sub == PER - 1:
-                    @pl.when(n + SLOTS < units)
-                    def _():
-                        load_down(n + SLOTS, slot)
-
-            b = n - LAG_B // PER
-
-            @pl.when((b >= 0) & (b < units))
-            def _():
+                load_down(n + SLOTS, slot_down(n))
+
+        b = n - LAG_B
+
+        @pl.when((b >= 0) & (b < units))
+        def _():
+            for sub in range(PER):
                 a_copy(b, sub).wait_recv()
                 total = keep(b, sub)[...] + a_in[PER * b + sub].astype(F32)
                 b_out(b, sub)[...] = total[rows:].astype(BF16)
                 mine(b, sub)[...] = total[:rows]
                 b_copy(b, sub).start()
 
-            c = n - LAG_C // PER
-
-            @pl.when((c >= 0) & (c < units))
-            def _():
+        c = n - LAG_C
+
+        @pl.when((c >= 0) & (c < units))
+        def _():
+            for sub in range(PER):
                 b_copy(c, sub).wait_recv()
                 c_out(c, sub)[...] = (mine(c, sub)[...] + b_in[PER * c + sub].astype(F32)).astype(BF16)
                 c_copy(c, sub).start()
 
-            d = n - LAG_D // PER
-
-            @pl.when(d >= 0)
-            def _():
+        d = n - LAG_D
+
+        @pl.when(d >= 0)
+        def _():
+            for sub in range(PER):
                 c_copy(d, sub).wait_recv()
                 m = PER * d + sub
                 d_cols(d, sub)[...] = (c_out(d, sub)[...].astype(F32) + c_in[m].astype(F32)).astype(BF16)
                 d_copy(d, sub).start()
 
-    loop(0, units + LAG_D // PER, finish)
+    loop(1, units + LAG_D, finish)
 
     whole = xb.at[:, :, pl.ds(0, PER * SUB)]
     pltpu.make_async_copy(whole, whole, a_send.at[0]).wait()

time: 107 us -> 105 us (0.981)
  Pallas kernels: 105 us -> 103 us
    pallas_call x1, Pallas kernels: 105 us -> 103 us  [step(): pl.pallas_call(kernel, out_shape=pltpu.VMEM((rows, depth), BF16), in_spec...]
where the time goes in v3:
time: 105 us
  Pallas kernels  103 us (98%)
  local copies, waits for them, and re-layouts  1.67 us (2%)
    pallas_call x1, Pallas kernels, step(): pl.pallas_call(kernel, out_shape=pltpu.VMEM((rows, depth), BF16), in_spec...  103 us

profile of v3, /device:TPU:0, one launch (start us, length us, event | category | flops | bytes accessed | tf_op | source)
XLA Modules:
  0.0 104.9 jit_solution(2179521987552074768)
XLA Ops:
  0.0 103.2 %shard_map.46 = bf16[128,12288]{1,0:T(8,128)(2,1)S(1)} custom-call(bf16[128,12288]{1,0:T(8,128)(2,1)} %x_ref.1, bf16[12288,7168]{1,0:T(8,128)(2,1)} %wg_ref.1, bf16[12288,7168]{1,0:T(8,128)(2,1)} %wu_ref.1, bf16[14,512,12288]{2,1,0:T(8,128)(2,1)} %bitcast.wd_ref), custom_call_target="tpu_custom_call" | custom-call | tf_op jit(solution)/shard_map/pallas_call | solution.py:306
  103.2 1.7 %copy.6 = bf16[128,12288]{1,0:T(8,128)(2,1)} copy(bf16[128,12288]{1,0:T(8,128)(2,1)S(1)} %shard_map.46) | data formatting | bytes 6291456

commit v4 on v3

--- a/solution.py
+++ b/solution.py
@@ -16,7 +16,7 @@
 SUB = 128
 PER = NC // (2 * SUB)
 SLOTS = 10
-EARLY = 3
+EARLY = 2
 SINGLES = 8
 LAG_B, LAG_C, LAG_D = 1, 4, 7
 RING_A, RING_B, RING_C = 8, 16, 16
@@ -197,11 +197,11 @@
     loop(0, EARLY, late)
 
     def single(s):
-        @pl.when(s + 2 < SINGLES)
-        def _():
-            take_x(s + 2, 1)
-
-        @pl.when(s + 2 == SINGLES)
+        @pl.when(s + EARLY - 1 < SINGLES)
+        def _():
+            take_x(s + EARLY - 1, 1)
+
+        @pl.when(s + EARLY - 1 == SINGLES)
         def _():
             take_x(SINGLES, 2)
 

time: 105 us -> 107 us (1.019)
  Pallas kernels: 103 us -> 105 us
    pallas_call x1, Pallas kernels: 103 us -> 105 us  [step(): pl.pallas_call(kernel, out_shape=pltpu.VMEM((rows, depth), BF16), in_spec...]
where the time goes in v4:
time: 107 us
  Pallas kernels  105 us (98%)
  local copies, waits for them, and re-layouts  1.67 us (2%)
    pallas_call x1, Pallas kernels, step(): pl.pallas_call(kernel, out_shape=pltpu.VMEM((rows, depth), BF16), in_spec...  105 us

profile of v4, /device:TPU:0, one launch (start us, length us, event | category | flops | bytes accessed | tf_op | source)
XLA Modules:
  0.0 106.6 jit_solution(3565662770166698298)
XLA Ops:
  0.0 104.9 %shard_map.46 = bf16[128,12288]{1,0:T(8,128)(2,1)S(1)} custom-call(bf16[128,12288]{1,0:T(8,128)(2,1)} %x_ref.1, bf16[12288,7168]{1,0:T(8,128)(2,1)} %wg_ref.1, bf16[12288,7168]{1,0:T(8,128)(2,1)} %wu_ref.1, bf16[14,512,12288]{2,1,0:T(8,128)(2,1)} %bitcast.wd_ref), custom_call_target="tpu_custom_call" | custom-call | tf_op jit(solution)/shard_map/pallas_call | solution.py:306
  104.9 1.7 %copy.6 = bf16[128,12288]{1,0:T(8,128)(2,1)} copy(bf16[128,12288]{1,0:T(8,128)(2,1)S(1)} %shard_map.46) | data formatting | bytes 6291456
